TPU v7x, 32 devices: a whole 2x2x4 slice. The times are simulated.
32 devices in a mesh: row: 8 (over z, core), col: 4 (over y, x).
Axes of the slice: x: 2, y: 2, z: 4, core: 2. Of those that a mesh axis runs over, the one named last changes fastest.
Arguments:
- genotypes: int32 [512, 16384], P(('row', 'col')), may hold values from 0 to 2, as said below
- snp_index: int32 [512], P(('row', 'col')), may hold values from 0 to 2047, as said below
- freq_table: float32 [2048], replicated, as said below
- prior: float32 [16384, 16384], P('row', 'col'), as said below
- start_vectors: float32 [16384, 20], P('row'), may hold values from -6 to 6
Outputs:
- grm: float32 [16384, 16384], P('row', 'col')
- pcs: float32 [16384, 20], P('col')
- spectrum: float32 [3, 20], replicated
Inputs may be any that keep to these rules, and one draw needn't show every extreme that they name: `genotypes`: genotype dosages 0, 1 or 2. `snp_index`: strictly increasing; entry j lies in 4 * j to 4 * j + 3. `freq_table`: frequencies are multiples of 1/1024 between 52/1024 and 512/1024. `prior`: exactly symmetric; diagonal between 1 and 2, off-diagonal entries small.
All inputs are finite; a program needn't handle non-finite values.
Results may differ from a plain program's by a relative error of at most 0.0075.
Values may be sent and summed in bfloat16 or wider, within the bound.
A program may use at most 128 MiB of HBM per device.

v0:
```python
import jax
import jax.numpy as jnp
from jax import lax
from jax.sharding import PartitionSpec as P

S = 16384
ITERS = 3


def standardize(genotypes, allele_freq):
    doubled = 2.0 * allele_freq
    spread = jnp.sqrt(doubled * (1.0 - allele_freq))
    return (genotypes.astype(jnp.float32) - doubled[:, None]) / spread[:, None]


def orthonormal(factor, image):
    return lax.linalg.triangular_solve(factor, image, left_side=False, lower=True, transpose_a=True)


def apply_tile(tile, vectors, transposed):
    if transposed:
        return lax.dot_general(
            tile, vectors, (((0,), (0,)), ((), ())), precision=lax.Precision.HIGHEST
        )
    return jnp.dot(tile, vectors, precision=lax.Precision.HIGHEST)


def local_gram(image):
    return jnp.dot(image.T, image, precision=lax.Precision.HIGHEST)


def body(genotypes, snp_index, freq_table, prior, start_vectors):
    allele_freq = jnp.take(freq_table, snp_index)
    standard = standardize(genotypes, allele_freq).astype(jnp.bfloat16)
    row_count = lax.axis_size("row")
    col_count = lax.axis_size("col")
    own_snps = genotypes.shape[0]
    total_snps = own_snps * row_count * col_count
    row_piece = lax.all_to_all(standard, "row", split_axis=1, concat_axis=0, tiled=True)
    col_piece = lax.all_to_all(standard, "col", split_axis=1, concat_axis=0, tiled=True)
    col_piece = col_piece.reshape(col_count, 1, own_snps, col_piece.shape[1])
    col_panel = lax.all_gather(col_piece, "row", axis=1, tiled=True)
    col_panel = col_panel.reshape(total_snps, col_panel.shape[3])
    window = lax.dot_general(
        lax.all_gather(row_piece, "col", axis=0, tiled=True),
        col_panel,
        (((0,), (0,)), ((), ())),
        preferred_element_type=jnp.float32,
    )
    grm = prior + window / total_snps
    scaled_start = start_vectors / jnp.sqrt(jnp.float32(S))
    diagonals = []
    image = lax.psum(apply_tile(grm, scaled_start, True), "row")
    for step in range(1, ITERS):
        if step % 2 == 1:
            product, gram = lax.psum((apply_tile(grm, image, False), local_gram(image)), "col")
        else:
            product, gram = lax.psum((apply_tile(grm, image, True), local_gram(image)), "row")
        factor = jnp.linalg.cholesky(gram)
        diagonals.append(jnp.diagonal(factor))
        image = orthonormal(factor, product)
    gram = lax.psum(local_gram(image), "col")
    factor = jnp.linalg.cholesky(gram)
    diagonals.append(jnp.diagonal(factor))
    vectors = orthonormal(factor, image)
    pcs = vectors * jnp.sqrt(jnp.float32(S))
    spectrum = jnp.stack(diagonals, axis=0)
    return (grm, pcs, spectrum)


def solution(mesh):
    return jax.shard_map(
        body,
        mesh=mesh,
        in_specs=(P(("row", "col"), None), P(("row", "col")), P(), P("row", "col"), P("row", None)),
        out_specs=(P("row", "col"), P("col", None), P()),
        check_vma=False,
    )
```

profile of v0, /device:TPU:0, one launch (start us, length us, event | category | flops | bytes accessed | tf_op | source)
XLA Modules:
  0.0 454.8 jit_solution(4961095967382614033)
XLA Ops:
  9.2 1.4 divide_convert_fusion
  10.7 13.5 %all_to_all.35 = bf16[16,4,4096]{2,0,1:T(8,128)(2,1)S(1)} all-to-all(bf16[16,4,4096]{2,0,1:T(8,128)(2,1)S(1)} %bitcast.73), channel_id=1, replica_groups=mesh['row'=8,'col'=4] {'col'}, dimensions={1} | all-to-all | bytes 1048576 | tf_op jit(solution)/shard_map/all_to_all | solution.py:40
  25.5 31.8 %all_to_all.36 = bf16[16,8,2048]{2,0,1:T(8,128)(2,1)} all-to-all(bf16[16,8,2048]{2,0,1:T(8,128)(2,1)S(1)} %bitcast.72), channel_id=1, replica_groups=mesh['row'=8,'col'=4] {'row'}, dimensions={1} | all-to-all | bytes 1048576 | tf_op jit(solution)/shard_map/all_to_all | solution.py:39
  57.4 23.7 %all-gather.6.cloned.1.call-done = bf16[4,128,4096]{2,0,1:T(4,128)(2,1)} async-done(((bf16[4,16,4096]{2,0,1:T(4,128)(2,1)}), bf16[4,128,4096]{2,0,1:T(4,128)(2,1)}) %all-gather.6.cloned.1.call-update) | async-done | bytes 4194320 | tf_op jit(solution)/shard_map/all_gather | solution.py:42
  81.1 6.5 %copy.31 = bf16[4,128,4096]{2,1,0:T(8,128)(2,1)} copy(bf16[4,128,4096]{2,0,1:T(4,128)(2,1)} %all-gather.6.cloned.1.call-done) | data formatting | bytes 8388608 | tf_op jit(solution)/shard_map/all_gather | solution.py:42
  87.5 28.0 %all-gather.4.cloned.1.call-done = bf16[512,2048]{1,0:T(8,128)(2,1)} async-done(((bf16[128,2048]{1,0:T(8,128)(2,1)}), bf16[512,2048]{1,0:T(8,128)(2,1)}) %all-gather.4.cloned.1.call-update) | async-done | bytes 2097168 | tf_op jit(solution)/shard_map/all_gather | solution.py:45
  115.5 28.8 %multiply_add_fusion = f32[2048,4096]{1,0:T(8,128)} fusion(f32[2048,4096]{1,0:T(8,128)} %param.11, bf16[512,2048]{1,0:T(8,128)(2,1)} %all-gather.4.cloned.1.call-done, bf16[512,4096]{1,0:T(8,128)(2,1)} %bitcast.67), kind=kOutput, calls=%fused_computation.4 | convolution fusion | flops 8606711808 | bytes 73400320 | tf_op jit(solution)/shard_map/dot_general | solution.py:44
  144.3 22.0 %fusion.1 = f32[4096,20]{0,1:T(8,128)} fusion(f32[2048,4096]{1,0:T(8,128)} %multiply_add_fusion, f32[2048,20]{0,1:T(8,128)S(1)} %copy-done.2), kind=kOutput, calls=%fused_computation.11 | convolution fusion | flops 2013306880 | bytes 34045952 | tf_op jit(solution)/shard_map/dot_general | solution.py:22
  166.4 55.9 %all-reduce.4.cloned.1.call-done = f32[4096,20]{0,1:T(8,128)} async-done(((f32[4096,20]{0,1:T(8,128)}), f32[4096,20]{0,1:T(8,128)}) %all-reduce.4.cloned.1.call-update) | async-done | bytes 327696 | tf_op jit(solution)/shard_map/psum | solution.py:53
  222.4 1.6 fusion.27
  224.0 15.9 %psum.44 = f32[20,20]{0,1:T(8,128)S(1)} all-reduce(f32[20,20]{0,1:T(8,128)S(1)} %fusion.27), channel_id=1, replica_groups=mesh['row'=8,'col'=4] {'col'}, use_global_device_ids=true, to_apply=%region_2.3 | all-reduce | flops 400 | bytes 3200 | tf_op jit(solution)/shard_map/psum | solution.py:56
  240.0 1.8 cholesky.59
  242.5 32.6 %fusion.26 = f32[2048,20]{0,1:T(8,128)} fusion(f32[2048,4096]{1,0:T(8,128)} %multiply_add_fusion, f32[4096,20]{0,1:T(8,128)} %all-reduce.4.cloned.1.call-done), kind=kOutput, calls=%fused_computation.50 | convolution fusion | flops 2013265920 | bytes 34045952 | tf_op jit(solution)/shard_map/dot_general | solution.py:25
  275.9 1.5 custom-call.8
  278.2 37.0 %all-reduce.6.cloned.1.call-done = f32[2048,20]{0,1:T(8,128)} async-done(((f32[2048,20]{0,1:T(8,128)}), f32[2048,20]{0,1:T(8,128)}) %all-reduce.6.cloned.1.call-update) | async-done | bytes 163856 | tf_op jit(solution)/shard_map/psum | solution.py:56
  316.8 22.0 %fusion.29 = f32[4096,20]{0,1:T(8,128)} fusion(f32[2048,4096]{1,0:T(8,128)} %multiply_add_fusion, f32[2048,20]{0,1:T(8,128)S(1)} %fusion.8), kind=kOutput, calls=%fused_computation.53 | convolution fusion | flops 2013265920 | bytes 34045952 | tf_op jit(solution)/shard_map/dot_general | solution.py:22
  338.8 28.1 %psum.45 = f32[20,20]{0,1:T(8,128)S(1)} all-reduce(f32[20,20]{0,1:T(8,128)S(1)} %fusion.28), channel_id=1, replica_groups=mesh['row'=8,'col'=4] {'row'}, use_global_device_ids=true, to_apply=%region_5.7 | all-reduce | flops 400 | bytes 3200 | tf_op jit(solution)/shard_map/psum | solution.py:58
  367.0 1.8 cholesky.70
  370.1 1.5 custom-call.16
  372.5 50.4 %all-reduce.8.cloned.1.call-done = f32[4096,20]{0,1:T(8,128)} async-done(((f32[4096,20]{0,1:T(8,128)}), f32[4096,20]{0,1:T(8,128)}) %all-reduce.8.cloned.1.call-update) | async-done | bytes 327696 | tf_op jit(solution)/shard_map/psum | solution.py:58
  422.9 1.5 convolution_bitcast_fusion.1
  424.9 15.9 %psum.47 = f32[20,20]{0,1:T(8,128)S(1)} all-reduce(f32[20,20]{0,1:T(8,128)S(1)} %fusion.30), channel_id=1, replica_groups=mesh['row'=8,'col'=4] {'col'}, use_global_device_ids=true, to_apply=%region_7.10 | all-reduce | flops 400 | bytes 3200 | tf_op jit(solution)/shard_map/psum | solution.py:62
  441.0 1.8 cholesky.81
  444.9 1.5 custom-call.17
  (48 shorter events, 14.2 us)
Async XLA Ops:
  7.2 0.7 copy-start
  7.2 73.9 %all-gather.6.cloned.1.call-start = ((), (), s32[]{:S(2)}) async-start(), calls=%async_computation.6 | async-start | bytes 4718592 | tf_op jit(solution)/shard_map/all_gather | solution.py:42
  25.4 90.0 %all-gather.4.cloned.1.call-start = ((), (), s32[]{:S(2)}) async-start(), calls=%async_computation.2 | async-start | bytes 2621440 | tf_op jit(solution)/shard_map/all_gather | solution.py:45
  57.3 165.1 %all-reduce.4.cloned.1.call-start = ((), (), s32[]{:S(2)}) async-start(), calls=%async_computation.3 | async-start | bytes 786432 | tf_op jit(solution)/shard_map/psum | solution.py:53
  115.5 28.8 %copy-start.2 = (f32[2048,20]{0,1:T(8,128)S(1)}, f32[2048,20]{0,1:T(8,128)}, u32[]{:S(2)}) copy-start(f32[2048,20]{0,1:T(8,128)} %param.12) | copy-start | bytes 491524
  166.4 148.8 %all-reduce.6.cloned.1.call-start = ((), (), s32[]{:S(2)}) async-start(), calls=%async_computation.4 | async-start | bytes 393216 | tf_op jit(solution)/shard_map/psum | solution.py:56
  242.5 205.8 %copy-start.1 = (f32[2048]{0:T(1024)S(1)}, f32[2048]{0:T(1024)}, u32[]{:S(2)}) copy-start(f32[2048]{0:T(1024)} %param.10) | copy-start | bytes 24580
  275.2 147.7 %all-reduce.8.cloned.1.call-start = ((), (), s32[]{:S(2)}) async-start(), calls=%async_computation.5 | async-start | bytes 786432 | tf_op jit(solution)/shard_map/psum | solution.py:58
Sparse Core Ops, SparseCore 0:
  25.5 55.4 all-gather.5
  82.9 32.5 all-gather.3
  166.5 55.8 all-reduce.3
  275.3 39.8 all-reduce.5
  369.6 53.2 all-reduce.7
where the time goes:
time: 455 us
  waiting for transfers between devices  195 us (43%)
  matrix products  112 us (25%)
  blocking collectives  105 us (23%)
  other arithmetic  17.4 us (4%)
  between operations  13.9 us (3%)
  local copies, waits for them, and re-layouts  11.1 us (2%)
    psum x1, waiting for transfers between devices, body(): image = lax.psum(apply_tile(grm, scaled_start, True), 'row')  55.9 us
    psum x1, waiting for transfers between devices, body(): lax.psum((apply_tile(grm, image, True), local_gram(image)), 'row')  50.4 us
    dot_general x2, matrix products, apply_tile(): lax.dot_general(tile, vectors, (((0,), (0,)), ((), ())), precision=lax.Pr...  44.1 us
    psum x1, waiting for transfers between devices, body(): lax.psum((apply_tile(grm, image, False), local_gram(image)), 'col')  37 us
    dot_general x1, matrix products, apply_tile(): return jnp.dot(tile, vectors, precision=lax.Precision.HIGHEST)  32.6 us
    all_to_all x1, blocking collectives, body(): lax.all_to_all(standard, 'row', split_axis=1, concat_axis=0, tiled=True)  31.8 us
    dot_general x1, matrix products, body(): lax.dot_general(lax.all_gather(row_piece, 'col', axis=0, tiled=True), col...  28.8 us
    psum x1, blocking collectives, body(): lax.psum((apply_tile(grm, image, True), local_gram(image)), 'row')  28.1 us
  transfers between devices with their start and end apart: 5, of which 5 were waited for; matrix products, arithmetic and copies ran while one was open for 3% of the time, Pallas kernels for 0%

commit v1 on v0

--- a/solution.py
+++ b/solution.py
@@ -36,7 +36,10 @@
     col_count = lax.axis_size("col")
     own_snps = genotypes.shape[0]
     total_snps = own_snps * row_count * col_count
-    row_piece = lax.all_to_all(standard, "row", split_axis=1, concat_axis=0, tiled=True)
+    row_piece = jnp.concatenate(
+        lax.all_to_all(jnp.stack(jnp.split(standard, lax.axis_size("row"), axis=1)), "row", 0, 0),
+        axis=0,
+    )
     col_piece = lax.all_to_all(standard, "col", split_axis=1, concat_axis=0, tiled=True)
     col_piece = col_piece.reshape(col_count, 1, own_snps, col_piece.shape[1])
     col_panel = lax.all_gather(col_piece, "row", axis=1, tiled=True)

time: 455 us -> 455 us (level)
  no operation moved by 1% of the time
where the time goes in v1:
time: 455 us
  waiting for transfers between devices  195 us (43%)
  matrix products  112 us (25%)
  blocking collectives  105 us (23%)
  other arithmetic  17.4 us (4%)
  between operations  13.9 us (3%)
  local copies, waits for them, and re-layouts  11.1 us (2%)
    psum x1, waiting for transfers between devices, body(): image = lax.psum(apply_tile(grm, scaled_start, True), 'row')  56 us
    psum x1, waiting for transfers between devices, body(): lax.psum((apply_tile(grm, image, True), local_gram(image)), 'row')  50.4 us
    dot_general x2, matrix products, apply_tile(): lax.dot_general(tile, vectors, (((0,), (0,)), ((), ())), precision=lax.Pr...  44.1 us
    psum x1, waiting for transfers between devices, body(): lax.psum((apply_tile(grm, image, False), local_gram(image)), 'col')  37 us
    dot_general x1, matrix products, apply_tile(): return jnp.dot(tile, vectors, precision=lax.Precision.HIGHEST)  32.6 us
    all_to_all x1, blocking collectives, body(): lax.all_to_all(jnp.stack(jnp.split(standard, lax.axis_size('row'), axis=1...  31.8 us
    dot_general x1, matrix products, body(): lax.dot_general(lax.all_gather(row_piece, 'col', axis=0, tiled=True), col...  28.8 us
    psum x1, blocking collectives, body(): lax.psum((apply_tile(grm, image, True), local_gram(image)), 'row')  28.1 us
  transfers between devices with their start and end apart: 5, of which 5 were waited for; matrix products, arithmetic and copies ran while one was open for 3% of the time, Pallas kernels for 0%

profile of v1, /device:TPU:0, one launch (start us, length us, event | category | flops | bytes accessed | tf_op | source)
XLA Modules:
  0.0 455.0 jit_solution(11869904122598946422)
XLA Ops:
  9.2 1.4 divide_convert_fusion
  10.7 13.5 %all_to_all.21 = bf16[16,4,4096]{2,0,1:T(8,128)(2,1)S(1)} all-to-all(bf16[16,4,4096]{2,0,1:T(8,128)(2,1)S(1)} %bitcast.97), channel_id=1, replica_groups=mesh['row'=8,'col'=4] {'col'}, dimensions={1} | all-to-all | bytes 1048576 | tf_op jit(solution)/shard_map/all_to_all | solution.py:43
  25.6 31.8 %all_to_all.22 = bf16[8,16,2048]{2,1,0:T(8,128)(2,1)} all-to-all(bf16[8,16,2048]{2,1,0:T(8,128)(2,1)S(1)} %fusion.4), channel_id=1, replica_groups=mesh['row'=8,'col'=4] {'row'}, dimensions={0} | all-to-all | bytes 1048576 | tf_op jit(solution)/shard_map/all_to_all | solution.py:40
  57.5 23.6 %all-gather.6.cloned.1.call-done = bf16[4,128,4096]{2,0,1:T(4,128)(2,1)} async-done(((bf16[4,16,4096]{2,0,1:T(4,128)(2,1)}), bf16[4,128,4096]{2,0,1:T(4,128)(2,1)}) %all-gather.6.cloned.1.call-update) | async-done | bytes 4194320 | tf_op jit(solution)/shard_map/all_gather | solution.py:45
  81.1 6.5 %copy.29 = bf16[4,128,4096]{2,1,0:T(8,128)(2,1)} copy(bf16[4,128,4096]{2,0,1:T(4,128)(2,1)} %all-gather.6.cloned.1.call-done) | data formatting | bytes 8388608 | tf_op jit(solution)/shard_map/all_gather | solution.py:45
  87.6 28.0 %all-gather.4.cloned.1.call-done = bf16[512,2048]{1,0:T(8,128)(2,1)} async-done(((bf16[128,2048]{1,0:T(8,128)(2,1)}), bf16[512,2048]{1,0:T(8,128)(2,1)}) %all-gather.4.cloned.1.call-update) | async-done | bytes 2097168 | tf_op jit(solution)/shard_map/all_gather | solution.py:48
  115.5 28.8 %multiply_add_fusion = f32[2048,4096]{1,0:T(8,128)} fusion(f32[2048,4096]{1,0:T(8,128)} %param.11, bf16[512,2048]{1,0:T(8,128)(2,1)} %all-gather.4.cloned.1.call-done, bf16[512,4096]{1,0:T(8,128)(2,1)} %bitcast.93), kind=kOutput, calls=%fused_computation.4 | convolution fusion | flops 8606711808 | bytes 73400320 | tf_op jit(solution)/shard_map/dot_general | solution.py:47
  144.4 22.0 %fusion.1 = f32[4096,20]{0,1:T(8,128)} fusion(f32[2048,4096]{1,0:T(8,128)} %multiply_add_fusion, f32[2048,20]{0,1:T(8,128)S(1)} %copy-done.2), kind=kOutput, calls=%fused_computation.10 | convolution fusion | flops 2013306880 | bytes 34045952 | tf_op jit(solution)/shard_map/dot_general | solution.py:22
  166.5 56.0 %all-reduce.4.cloned.1.call-done = f32[4096,20]{0,1:T(8,128)} async-done(((f32[4096,20]{0,1:T(8,128)}), f32[4096,20]{0,1:T(8,128)}) %all-reduce.4.cloned.1.call-update) | async-done | bytes 327696 | tf_op jit(solution)/shard_map/psum | solution.py:56
  222.5 1.6 fusion.35
  224.2 15.9 %psum.44 = f32[20,20]{0,1:T(8,128)S(1)} all-reduce(f32[20,20]{0,1:T(8,128)S(1)} %fusion.35), channel_id=1, replica_groups=mesh['row'=8,'col'=4] {'col'}, use_global_device_ids=true, to_apply=%region_2.3 | all-reduce | flops 400 | bytes 3200 | tf_op jit(solution)/shard_map/psum | solution.py:59
  240.2 1.8 cholesky.59
  242.7 32.6 %fusion.34 = f32[2048,20]{0,1:T(8,128)} fusion(f32[2048,4096]{1,0:T(8,128)} %multiply_add_fusion, f32[4096,20]{0,1:T(8,128)} %all-reduce.4.cloned.1.call-done), kind=kOutput, calls=%fused_computation.65 | convolution fusion | flops 2013265920 | bytes 34045952 | tf_op jit(solution)/shard_map/dot_general | solution.py:25
  276.0 1.5 custom-call.8
  278.4 37.0 %all-reduce.6.cloned.1.call-done = f32[2048,20]{0,1:T(8,128)} async-done(((f32[2048,20]{0,1:T(8,128)}), f32[2048,20]{0,1:T(8,128)}) %all-reduce.6.cloned.1.call-update) | async-done | bytes 163856 | tf_op jit(solution)/shard_map/psum | solution.py:59
  316.9 22.0 %fusion.37 = f32[4096,20]{0,1:T(8,128)} fusion(f32[2048,4096]{1,0:T(8,128)} %multiply_add_fusion, f32[2048,20]{0,1:T(8,128)S(1)} %fusion.16), kind=kOutput, calls=%fused_computation.68 | convolution fusion | flops 2013265920 | bytes 34045952 | tf_op jit(solution)/shard_map/dot_general | solution.py:22
  339.0 28.1 %psum.45 = f32[20,20]{0,1:T(8,128)S(1)} all-reduce(f32[20,20]{0,1:T(8,128)S(1)} %fusion.36), channel_id=1, replica_groups=mesh['row'=8,'col'=4] {'row'}, use_global_device_ids=true, to_apply=%region_5.7 | all-reduce | flops 400 | bytes 3200 | tf_op jit(solution)/shard_map/psum | solution.py:61
  367.1 1.8 cholesky.70
  370.3 1.5 custom-call.16
  372.6 50.4 %all-reduce.8.cloned.1.call-done = f32[4096,20]{0,1:T(8,128)} async-done(((f32[4096,20]{0,1:T(8,128)}), f32[4096,20]{0,1:T(8,128)}) %all-reduce.8.cloned.1.call-update) | async-done | bytes 327696 | tf_op jit(solution)/shard_map/psum | solution.py:61
  423.0 1.5 convolution_bitcast_fusion.1
  425.1 15.9 %psum.47 = f32[20,20]{0,1:T(8,128)S(1)} all-reduce(f32[20,20]{0,1:T(8,128)S(1)} %fusion.38), channel_id=1, replica_groups=mesh['row'=8,'col'=4] {'col'}, use_global_device_ids=true, to_apply=%region_7.10 | all-reduce | flops 400 | bytes 3200 | tf_op jit(solution)/shard_map/psum | solution.py:65
  441.1 1.8 cholesky.81
  445.0 1.5 custom-call.17
  (55 shorter events, 14.3 us)
Async XLA Ops:
  7.2 0.7 copy-start
  7.2 73.9 %all-gather.6.cloned.1.call-start = ((), (), s32[]{:S(2)}) async-start(), calls=%async_computation.6 | async-start | bytes 4718592 | tf_op jit(solution)/shard_map/all_gather | solution.py:45
  25.4 90.1 %all-gather.4.cloned.1.call-start = ((), (), s32[]{:S(2)}) async-start(), calls=%async_computation.2 | async-start | bytes 2621440 | tf_op jit(solution)/shard_map/all_gather | solution.py:48
  57.4 165.1 %all-reduce.4.cloned.1.call-start = ((), (), s32[]{:S(2)}) async-start(), calls=%async_computation.3 | async-start | bytes 786432 | tf_op jit(solution)/shard_map/psum | solution.py:56
  115.5 28.8 %copy-start.2 = (f32[2048,20]{0,1:T(8,128)S(1)}, f32[2048,20]{0,1:T(8,128)}, u32[]{:S(2)}) copy-start(f32[2048,20]{0,1:T(8,128)} %param.12) | copy-start | bytes 491524
  166.4 148.9 %all-reduce.6.cloned.1.call-start = ((), (), s32[]{:S(2)}) async-start(), calls=%async_computation.4 | async-start | bytes 393216 | tf_op jit(solution)/shard_map/psum | solution.py:59
  242.7 205.8 %copy-start.1 = (f32[2048]{0:T(1024)S(1)}, f32[2048]{0:T(1024)}, u32[]{:S(2)}) copy-start(f32[2048]{0:T(1024)} %param.10) | copy-start | bytes 24580
  275.3 147.7 %all-reduce.8.cloned.1.call-start = ((), (), s32[]{:S(2)}) async-start(), calls=%async_computation.5 | async-start | bytes 786432 | tf_op jit(solution)/shard_map/psum | solution.py:61
Sparse Core Ops, SparseCore 0:
  25.5 55.5 all-gather.5
  83.0 32.5 all-gather.3
  166.6 55.9 all-reduce.3
  275.4 39.8 all-reduce.5
  369.8 53.2 all-reduce.7
